TPU v7x, 32 devices: a whole 2x2x4 slice. The times are simulated.
32 devices in a mesh: lev: 4 (over x, core), lon: 8 (over z, y).
Axes of the slice: x: 2, y: 2, z: 4, core: 2. Of those that a mesh axis runs over, the one named last changes fastest.
Arguments:
- previous: float32 [36, 64, 4096], P('lev', None, 'lon'), may hold values from -4 to 4
- loss_matrix: float32 [36, 64, 64], P('lev'), may hold values from -3 to 10, as said below
- pair_matrix: float32 [36, 64, 64], P('lev'), may hold values from -0.1875 to 0.1875
- diffusivity: float32 [36], P('lev'), may hold values from 200 to 2000
- mixing: float32 [36], P('lev'), may hold values from 0.1 to 1
Outputs:
- concentration: float32 [36, 64, 4096], P('lev', None, 'lon')
- level_variance: float32 [36, 64], P('lev')
Inputs may be any that keep to these rules, and one draw needn't show every extreme that they name: `loss_matrix`: each of the 36 blocks is symmetric and at least 0.05 times the identity in the positive definite order.
All inputs are finite; a program needn't handle non-finite values.
Results may differ from a plain program's by a relative error of at most 0.00045.
Values sent between devices are 32-bit elements; how exact they have to be, the bound alone decides.
A program may use at most 64 MiB of HBM per device.

v0:
```python
import functools

import jax
import jax.numpy as jnp
from jax import lax
from jax.experimental import pallas as pl
from jax.experimental.pallas import tpu as pltpu
from jax.sharding import PartitionSpec as P

ITERS = 2
HIGHEST = lax.Precision.HIGHEST
SMEM = pl.BlockSpec(memory_space=pltpu.SMEM)
VMEM = pl.BlockSpec(memory_space=pltpu.VMEM)


def dot(a, b, dims=((1,), (0,))):
    return lax.dot_general(
        a, b, (dims, ((), ())), precision=HIGHEST, preferred_element_type=jnp.float32
    )


def dot_t(a, b):
    return dot(a, b, ((1,), (1,)))


def eye_of(size):
    rows = lax.broadcasted_iota(jnp.int32, (size, size), 0)
    cols = lax.broadcasted_iota(jnp.int32, (size, size), 1)
    return rows == cols


def invert_all(blocks):
    size = blocks[0].shape[0]
    on_diag = eye_of(size)
    unit = jnp.where(on_diag, 1.0, 0.0).astype(jnp.float32)
    start, worst = [], None
    for a in blocks:
        total = jnp.sum(jnp.abs(a), axis=0, keepdims=True)
        diag = jnp.sum(jnp.where(on_diag, a, 0.0), axis=0, keepdims=True)
        hi = jnp.max(total)
        lo = jnp.maximum(jnp.min(2.0 * diag - total), 1.0)
        scale = 2.0 / (hi + lo)
        rho = (hi - lo) / (hi + lo)
        start.append(scale * (2.0 * unit - scale * a))
        worst = rho if worst is None else jnp.maximum(worst, rho)

    def go_on(carry):
        return carry[0] > 3e-8

    def step(carry):
        bound, *xs = carry
        rest = [unit - dot(a, x) for a, x in zip(blocks, xs)]
        return (bound * bound, *[x + dot(x, r) for x, r in zip(xs, rest)])

    return lax.while_loop(go_on, step, (worst * worst, *start))[1:]


def plan(lo, hi, out):
    if lo >= hi:
        return 0
    mid = lo + (hi - lo) // 2
    depth = 1 + max(plan(lo, mid, out), plan(mid + 1, hi, out))
    out.setdefault(depth, []).append((lo, mid, hi))
    return depth


def dense_inverse(diag, low):
    count, size = len(diag), diag[0].shape[0]
    unit = jnp.where(eye_of(size), 1.0, 0.0).astype(jnp.float32)
    by_depth, done = {}, {}
    plan(0, count, by_depth)
    for depth in sorted(by_depth):
        nodes = by_depth[depth]
        schur, arms = [], []
        for lo, mid, hi in nodes:
            s, parts = diag[mid], []
            if lo < mid:
                panel = done[lo, mid][-1]
                arm = low_right(panel, low, mid, False)
                s = s - low(mid, arm[-size:])
                parts.append(arm)
            parts.append(unit)
            if mid + 1 < hi:
                panel = done[mid + 1, hi][0]
                arm = low_right(panel, low, mid + 1, True)
                s = s - low(mid + 1, arm[:size], True)
                parts.append(arm)
            schur.append(s)
            arms.append(jnp.concatenate(parts, axis=0) if len(parts) > 1 else parts[0])
        for (lo, mid, hi), v, z in zip(nodes, arms, invert_all(schur)):
            if hi - lo == 1:
                done[lo, hi] = [z]
                continue
            w = dot(v, z)
            panels = []
            for k in range(lo, hi):
                vk = v[(k - lo) * size : (k - lo + 1) * size]
                new = w if k == mid else dot_t(w, vk)
                pieces = []
                for a, b in ((lo, mid), (mid, mid + 1), (mid + 1, hi)):
                    if a >= b:
                        continue
                    piece = new[(a - lo) * size : (b - lo) * size]
                    if a <= k < b and k != mid:
                        piece = piece + done[a, b][k - a]
                    pieces.append(piece)
                panels.append(jnp.concatenate(pieces, axis=0) if len(pieces) > 1 else pieces[0])
            done[lo, hi] = panels
    return done[0, count]


def low_right(panel, low, k, plain):
    return low(k, panel, not plain, True)


def split(x):
    high = x.astype(jnp.bfloat16)
    return high, (x - high.astype(jnp.float32)).astype(jnp.bfloat16)


def dot3(a_high, a_low, b):
    b_high, b_low = split(b)
    mul = functools.partial(jnp.dot, preferred_element_type=jnp.float32)
    return mul(a_high, b_high) + (mul(a_low, b_high) + mul(a_high, b_low))


def factor_kernel(links_ref, loss_ref, high_ref, low_ref, ends_ref, send_ref):
    levels, size = loss_ref.shape[0], loss_ref.shape[1]
    inner = levels - 1
    on_diag = eye_of(size)

    def diag_of(k):
        return loss_ref[k] + jnp.where(on_diag, 1.0 + links_ref[k] + links_ref[k + 1], 0.0)

    def low(k, x, transposed=False, right=False):
        return links_ref[k] * x

    panels = dense_inverse([diag_of(k) for k in range(inner)], low)
    top_link, inner_link = links_ref[0], links_ref[inner]
    for k, panel in enumerate(panels):
        high, rest = split(panel)
        high_ref[:, k * size : (k + 1) * size] = high
        low_ref[:, k * size : (k + 1) * size] = rest
    ends_ref[0] = top_link * panels[0]
    ends_ref[1] = inner_link * panels[-1]
    send_ref[0] = diag_of(inner) - inner_link * inner_link * panels[-1][-size:]
    send_ref[1] = top_link * top_link * panels[0][:size]
    send_ref[2] = inner_link * top_link * panels[0][-size:]


def interface_kernel(place_ref, all_ref, ends_ref, high_ref, low_ref, rows_ref):
    count, size = all_ref.shape[0], all_ref.shape[2]
    diag = [
        all_ref[k, 0] - all_ref[k + 1, 1] if k + 1 < count else all_ref[k, 0]
        for k in range(count)
    ]

    def low(k, x, transposed=False, right=False):
        block = all_ref[k, 2]
        if right:
            return dot_t(x, block) if transposed else dot(x, block)
        return dot(block, x, ((0,), (0,))) if transposed else dot(block, x)

    for k, panel in enumerate(dense_inverse(diag, low)):
        rows_ref[k] = panel
    me = place_ref[0]
    own = rows_ref[me]
    above = rows_ref[jnp.maximum(me - 1, 0)]
    inner = dot_t(ends_ref[0], above) + dot_t(ends_ref[1], own)
    length = inner.shape[0]
    high_ref[:length], low_ref[:length] = split(inner)
    high_ref[length:], low_ref[length:] = split(own.T)


def forcing_kernel(
    links_ref, mix_ref, cur_ref, left_ref, right_ref, prev_ref, pair_ref, high_ref, low_ref,
    part_ref, side_ref, top_ref, force_ref,
):
    levels, size, columns = cur_ref.shape
    lane = lax.broadcasted_iota(jnp.int32, (size, columns), 1)
    for k in range(levels):
        c = cur_ref[k]
        back = jnp.where(lane == 0, left_ref[k], pltpu.roll(c, 1, 1))
        ahead = jnp.where(lane == columns - 1, right_ref[k], pltpu.roll(c, columns - 1, 1))
        p_high, p_low = split(pair_ref[k])
        chem = dot3(p_high, p_low, c * c)
        force_ref[k * size : (k + 1) * size] = (
            prev_ref[k] - chem + mix_ref[k] * (back + ahead - 2.0 * c)
        )
    inner = (levels - 1) * size
    part = dot3(high_ref[...], low_ref[...], force_ref[:inner])
    part_ref[...] = part
    side_ref[...] = force_ref[inner:] + links_ref[levels - 1] * part[-size:]
    top_ref[...] = links_ref[0] * part[:size]


def finish_kernel(part_ref, sides_ref, high_ref, low_ref, out_ref, sum_ref):
    levels, size, columns = out_ref.shape
    inner = (levels - 1) * size
    x = dot3(high_ref[...], low_ref[...], sides_ref[...])
    for k in range(levels):
        row = x[k * size : (k + 1) * size]
        if k < levels - 1:
            row = row + part_ref[k * size : (k + 1) * size]
        out_ref[k] = row
        sum_ref[k] = jnp.sum(row * row, axis=1, keepdims=True)


def call(kernel, outs, places, scratch=()):
    return pl.pallas_call(
        kernel,
        out_shape=[jax.ShapeDtypeStruct(shape, dtype) for shape, dtype in outs],
        in_specs=places,
        out_specs=[VMEM] * len(outs),
        scratch_shapes=list(scratch),
        compiler_params=pltpu.CompilerParams(vmem_limit_bytes=60 * 2**20),
    )


def local(previous, loss_matrix, pair_matrix, diffusivity, mixing):
    levels, size, columns = previous.shape
    count = lax.axis_size("lev")
    around = lax.axis_size("lon")
    inner = (levels - 1) * size
    f32, bf16 = jnp.float32, jnp.bfloat16
    top_link = lax.ppermute(
        diffusivity[levels - 1 :], "lev", [(i, i + 1) for i in range(count - 1)]
    )
    links = jnp.concatenate([top_link, diffusivity])
    place = lax.axis_index("lev").astype(jnp.int32).reshape(1)
    g_high, g_low, ends, sent = call(
        factor_kernel,
        [((inner, inner), bf16), ((inner, inner), bf16), ((2, inner, size), f32), ((3, size, size), f32)],
        [SMEM, VMEM],
    )(links, loss_matrix)
    gathered = lax.all_gather(sent, "lev", axis=0)
    h_high, h_low = call(
        interface_kernel,
        [((levels * size, count * size), bf16)] * 2,
        [SMEM, VMEM, VMEM],
        [pltpu.VMEM((count, count * size, size), f32)],
    )(place, gathered, ends)
    current = previous
    for _ in range(ITERS):
        left = lax.ppermute(
            current[:, :, columns - 1 :], "lon", [(i, (i + 1) % around) for i in range(around)]
        )
        right = lax.ppermute(
            current[:, :, :1], "lon", [((i + 1) % around, i) for i in range(around)]
        )
        part, side, top = call(
            forcing_kernel,
            [((inner, columns), f32), ((size, columns), f32), ((size, columns), f32)],
            [SMEM, SMEM] + [VMEM] * 7,
            [pltpu.VMEM((levels * size, columns), f32)],
        )(links, mixing, current, left, right, previous, pair_matrix, g_high, g_low)
        side = side + lax.ppermute(top, "lev", [(i + 1, i) for i in range(count - 1)])
        sides = lax.all_gather(side, "lev", axis=0, tiled=True)
        current, squares = call(
            finish_kernel,
            [((levels, size, columns), f32), ((levels, size, 1), f32)],
            [VMEM] * 4,
        )(part, sides, h_high, h_low)
    totals = jnp.sum(lax.all_gather(squares[:, :, 0], "lon", axis=0), axis=0)
    return (current, totals / (columns * around))


def solution(mesh):
    placed = (P("lev", None, "lon"), P("lev", None, None), P("lev", None, None), P("lev"), P("lev"))
    return jax.shard_map(
        local,
        mesh=mesh,
        in_specs=placed,
        out_specs=(P("lev", None, "lon"), P("lev", None)),
        check_vma=False,
    )
```

profile of v0, /device:TPU:0, one launch (start us, length us, event | category | flops | bytes accessed | tf_op | source)
XLA Modules:
  0.0 133.3 jit_solution(3452445749497241001)
XLA Ops:
  0.6 1.3 slice.15
  1.9 2.9 %collective-permute-start = (f32[1]{0:T(128)}, f32[1]{0:T(128)}, u32[]{:S(2)}, u32[]{:S(2)}) collective-permute-start(f32[1]{0:T(128)} %slice.15), channel_id=1, source_target_pairs={{0,8},{8,16},{16,24},{1,9},{9,17},{17,25},{2,10},{10,18},{18,26},{... | collective-permute-start | bytes 20 | tf_op jit(solution)/shard_map/ppermute | solution.py:226
  4.9 1.2 fusion.1
  6.1 2.4 %collective-permute-start.1 = (f32[9,64,1]{2,1,0:T(8,128)S(1)}, f32[9,64,1]{2,1,0:T(8,128)S(1)}, u32[]{:S(2)}, u32[]{:S(2)}) collective-permute-start(f32[9,64,1]{2,1,0:T(8,128)S(1)} %get-tuple-element.35), channel_id=1, source_target_pairs={{0,1},{1,2},{2,3},{3,4},{4,5},{5,6},{6,7},{7,0},{8,9},{9,10},{10,1... | collective-permute-start | bytes 6920 | tf_op jit(solution)/shard_map/ppermute | solution.py:245
  8.4 3.1 %collective-permute-start.2 = (f32[9,64,1]{2,1,0:T(8,128)S(1)}, f32[9,64,1]{2,1,0:T(8,128)S(1)}, u32[]{:S(2)}, u32[]{:S(2)}) collective-permute-start(f32[9,64,1]{2,1,0:T(8,128)S(1)} %get-tuple-element.34), channel_id=1, source_target_pairs={{1,0},{2,1},{3,2},{4,3},{5,4},{6,5},{7,6},{0,7},{9,8},{10,9},{11,1... | collective-permute-start | bytes 6920 | tf_op jit(solution)/shard_map/ppermute | solution.py:248
  11.6 1.2 pad_maximum_fusion.links_ref
  12.8 10.3 %shard_map.68 = (bf16[512,512]{1,0:T(8,128)(2,1)}, bf16[512,512]{1,0:T(8,128)(2,1)}, f32[2,512,64]{2,1,0:T(8,128)}, f32[3,64,64]{2,1,0:T(8,128)}) custom-call(f32[10]{0:T(128)} %pad_maximum_fusion.links_ref, f32[9,64,64]{2,1,0:T(8,128)} %loss_ref.1), custom_call_target="tpu_custom_call" | custom-call | tf_op jit(solution)/shard_map/pallas_call | solution.py:231
  23.1 1.6 %collective-permute-done.2.right_ref = f32[9,64,1]{2,1,0:T(8,128)S(1)} collective-permute-done((f32[9,64,1]{2,1,0:T(8,128)S(1)}, f32[9,64,1]{2,1,0:T(8,128)S(1)}, u32[]{:S(2)}, u32[]{:S(2)}) %collective-permute-start.2) | collective-permute-done | bytes 2336 | tf_op jit(solution)/shard_map/ppermute | solution.py:248
  25.4 5.0 %shard_map.69 = (f32[512,512]{1,0:T(8,128)}, f32[64,512]{1,0:T(8,128)}, f32[64,512]{1,0:T(8,128)}) custom-call(f32[10]{0:T(128)} %pad_maximum_fusion.links_ref, f32[9]{0:T(128)} %mix_ref.3, f32[9,64,512]{2,1,0:T(8,128)} %prev_ref.3, f32[9,64,1]{2,1,0:T(8,128)} %copy-done, f32[9,64,1]{2,1,0:T(8,128)} %copy-done.1, f32[9,64,512]{2,1,0:T(8,128)} %prev_ref.3, ...), custom_call_target="tpu_custom_call" | custom-call | tf_op jit(solution)/shard_map/pallas_call | solution.py:251
  30.4 1.4 %collective-permute-start.3 = (f32[64,512]{1,0:T(8,128)}, f32[64,512]{1,0:T(8,128)S(1)}, u32[]{:S(2)}, u32[]{:S(2)}) collective-permute-start(f32[64,512]{1,0:T(8,128)} %get-tuple-element.21), channel_id=1, source_target_pairs={{8,0},{16,8},{24,16},{9,1},{17,9},{25,17},{10,2},{18,10},{26,18},{... | collective-permute-start | bytes 393224 | tf_op jit(solution)/shard_map/ppermute | solution.py:257
  31.8 8.9 %all-gather = f32[12,64,64]{2,1,0:T(8,128)} all-gather(f32[3,64,64]{2,1,0:T(8,128)S(1)} %copy-done.5), channel_id=2, replica_groups=mesh['lev'=4,'lon'=8] {'lev'}, dimensions={0}, use_global_device_ids=true | all-gather | bytes 245760 | tf_op jit(solution)/shard_map/all_gather | solution.py:236
  40.7 8.9 %shard_map.70 = (bf16[576,256]{1,0:T(8,128)(2,1)}, bf16[576,256]{1,0:T(8,128)(2,1)}) custom-call(s32[1]{0:T(128)} %bitcast.place_ref, f32[4,3,64,64]{3,2,1,0:T(8,128)} %bitcast.4, f32[2,512,64]{2,1,0:T(8,128)} %get-tuple-element.23.ends_ref), custom_call_target="tpu_custom_call" | custom-call | tf_op jit(solution)/shard_map/pallas_call | solution.py:237
  49.6 7.7 %all_gather.15.sides_ref = f32[256,512]{1,0:T(8,128)} all-gather(f32[64,512]{1,0:T(8,128)S(1)} %add.6), channel_id=1, replica_groups=mesh['lev'=4,'lon'=8] {'lev'}, dimensions={0}, use_global_device_ids=true | all-gather | bytes 655360 | tf_op jit(solution)/shard_map/all_gather | solution.py:258
  57.3 3.3 %shard_map.71 = (f32[9,64,512]{2,1,0:T(8,128)}, f32[9,64,1]{2,1,0:T(8,128)}) custom-call(f32[512,512]{1,0:T(8,128)} %get-tuple-element.19.part_ref, f32[256,512]{1,0:T(8,128)} %all_gather.15.sides_ref, bf16[576,256]{1,0:T(8,128)(2,1)} %get-tuple-element.24.high_ref, bf16[576,256]{1,0:T(8,128)(2,1)} %get-tuple-element.25.low_ref), custom_call_target="tpu_custom_call" | custom-call | tf_op jit(solution)/shard_map/pallas_call | solution.py:259
  60.6 1.2 fusion
  61.9 4.7 %collective-permute-start.5 = (f32[9,64,1]{2,1,0:T(8,128)S(1)}, f32[9,64,1]{2,1,0:T(8,128)S(1)}, u32[]{:S(2)}, u32[]{:S(2)}) collective-permute-start(f32[9,64,1]{2,1,0:T(8,128)S(1)} %get-tuple-element.32), channel_id=1, source_target_pairs={{1,0},{2,1},{3,2},{4,3},{5,4},{6,5},{7,6},{0,7},{9,8},{10,9},{11,1... | collective-permute-start | bytes 6920 | tf_op jit(solution)/shard_map/ppermute | solution.py:248
  66.6 8.7 %collective-permute-done.4.left_ref = f32[9,64,1]{2,1,0:T(8,128)S(1)} collective-permute-done((f32[9,64,1]{2,1,0:T(8,128)S(1)}, f32[9,64,1]{2,1,0:T(8,128)S(1)}, u32[]{:S(2)}, u32[]{:S(2)}) %collective-permute-start.4) | collective-permute-done | bytes 2336 | tf_op jit(solution)/shard_map/ppermute | solution.py:245
  75.2 2.6 %collective-permute-done.5.right_ref = f32[9,64,1]{2,1,0:T(8,128)S(1)} collective-permute-done((f32[9,64,1]{2,1,0:T(8,128)S(1)}, f32[9,64,1]{2,1,0:T(8,128)S(1)}, u32[]{:S(2)}, u32[]{:S(2)}) %collective-permute-start.5) | collective-permute-done | bytes 2336 | tf_op jit(solution)/shard_map/ppermute | solution.py:248
  78.6 5.0 %shard_map.72 = (f32[512,512]{1,0:T(8,128)}, f32[64,512]{1,0:T(8,128)}, f32[64,512]{1,0:T(8,128)}) custom-call(f32[10]{0:T(128)} %pad_maximum_fusion.links_ref, f32[9]{0:T(128)} %mix_ref.3, f32[9,64,512]{2,1,0:T(8,128)} %get-tuple-element.26.cur_ref, f32[9,64,1]{2,1,0:T(8,128)} %copy-done.2, f32[9,64,1]{2,1,0:T(8,128)} %copy-done.3, f32[9,64,512]{2,1,0:T(8,128)} %prev_ref.3, ...), custom_call_target="tpu_custom_call" | custom-call | tf_op jit(solution)/shard_map/pallas_call | solution.py:251
  83.6 1.3 collective-permute-start.6
  84.9 2.2 %collective-permute-done.6 = f32[64,512]{1,0:T(8,128)S(1)} collective-permute-done((f32[64,512]{1,0:T(8,128)}, f32[64,512]{1,0:T(8,128)S(1)}, u32[]{:S(2)}, u32[]{:S(2)}) %collective-permute-start.6) | collective-permute-done | bytes 131104 | tf_op jit(solution)/shard_map/ppermute | solution.py:257
  88.0 8.4 %all_gather.18.sides_ref = f32[256,512]{1,0:T(8,128)} all-gather(f32[64,512]{1,0:T(8,128)S(1)} %add.7), channel_id=1, replica_groups=mesh['lev'=4,'lon'=8] {'lev'}, dimensions={0}, use_global_device_ids=true | all-gather | bytes 655360 | tf_op jit(solution)/shard_map/all_gather | solution.py:258
  96.4 3.3 %shard_map.73 = (f32[9,64,512]{2,1,0:T(8,128)}, f32[9,64,1]{2,1,0:T(8,128)}) custom-call(f32[512,512]{1,0:T(8,128)} %get-tuple-element.27.part_ref, f32[256,512]{1,0:T(8,128)} %all_gather.18.sides_ref, bf16[576,256]{1,0:T(8,128)(2,1)} %get-tuple-element.24.high_ref, bf16[576,256]{1,0:T(8,128)(2,1)} %get-tuple-element.25.low_ref), custom_call_target="tpu_custom_call" | custom-call | tf_op jit(solution)/shard_map/pallas_call | solution.py:259
  100.7 30.7 %all-gather.1 = f32[72,64,1]{1,2,0:T(1,128)S(1)} all-gather(f32[9,64,1]{1,2,0:T(1,128)S(1)} %copy.7), channel_id=3, replica_groups=mesh['lev'=4,'lon'=8] {'lon'}, dimensions={0}, use_global_device_ids=true | all-gather | bytes 20736 | tf_op jit(solution)/shard_map/all_gather | solution.py:264
  (26 shorter events, 5.4 us)
Async XLA Ops:
  0.6 10.9 %copy-start.6 = (f32[9]{0:T(128)S(1)}, f32[9]{0:T(128)}, u32[]{:S(2)}) copy-start(f32[9]{0:T(128)} %param.8) | copy-start | bytes 112
  1.9 9.6 %collective-permute-start = (f32[1]{0:T(128)}, f32[1]{0:T(128)}, u32[]{:S(2)}, u32[]{:S(2)}) collective-permute-start(f32[1]{0:T(128)} %slice.15), channel_id=1, source_target_pairs={{0,8},{8,16},{16,24},{1,9},{9,17},{17,25},{2,10},{10,18},{18,26},{... | collective-permute-start | bytes 20 | tf_op jit(solution)/shard_map/ppermute | solution.py:226
  6.1 17.0 %collective-permute-start.1 = (f32[9,64,1]{2,1,0:T(8,128)S(1)}, f32[9,64,1]{2,1,0:T(8,128)S(1)}, u32[]{:S(2)}, u32[]{:S(2)}) collective-permute-start(f32[9,64,1]{2,1,0:T(8,128)S(1)} %get-tuple-element.35), channel_id=1, source_target_pairs={{0,1},{1,2},{2,3},{3,4},{4,5},{5,6},{6,7},{7,0},{8,9},{9,10},{10,1... | collective-permute-start | bytes 6920 | tf_op jit(solution)/shard_map/ppermute | solution.py:245
  8.4 16.2 %collective-permute-start.2 = (f32[9,64,1]{2,1,0:T(8,128)S(1)}, f32[9,64,1]{2,1,0:T(8,128)S(1)}, u32[]{:S(2)}, u32[]{:S(2)}) collective-permute-start(f32[9,64,1]{2,1,0:T(8,128)S(1)} %get-tuple-element.34), channel_id=1, source_target_pairs={{1,0},{2,1},{3,2},{4,3},{5,4},{6,5},{7,6},{0,7},{9,8},{10,9},{11,1... | collective-permute-start | bytes 6920 | tf_op jit(solution)/shard_map/ppermute | solution.py:248
  23.0 1.6 %copy-start = (f32[9,64,1]{2,1,0:T(8,128)}, f32[9,64,1]{2,1,0:T(8,128)S(1)}, u32[]{:S(2)}) copy-start(f32[9,64,1]{2,1,0:T(8,128)S(1)} %collective-permute-done.1.left_ref) | copy-start | bytes 6916
  24.6 0.7 copy-start.1
  25.4 6.5 %copy-start.5 = (f32[3,64,64]{2,1,0:T(8,128)S(1)}, f32[3,64,64]{2,1,0:T(8,128)}, u32[]{:S(2)}) copy-start(f32[3,64,64]{2,1,0:T(8,128)} %get-tuple-element.22) | copy-start | bytes 147460
  30.4 19.2 %copy-start.4 = (f32[64,512]{1,0:T(8,128)S(1)}, f32[64,512]{1,0:T(8,128)}, u32[]{:S(2)}) copy-start(f32[64,512]{1,0:T(8,128)} %get-tuple-element.20) | copy-start | bytes 393220
  30.4 19.2 %collective-permute-start.3 = (f32[64,512]{1,0:T(8,128)}, f32[64,512]{1,0:T(8,128)S(1)}, u32[]{:S(2)}, u32[]{:S(2)}) collective-permute-start(f32[64,512]{1,0:T(8,128)} %get-tuple-element.21), channel_id=1, source_target_pairs={{8,0},{16,8},{24,16},{9,1},{17,9},{25,17},{10,2},{18,10},{26,18},{... | collective-permute-start | bytes 393224 | tf_op jit(solution)/shard_map/ppermute | solution.py:257
  61.8 13.4 %collective-permute-start.4 = (f32[9,64,1]{2,1,0:T(8,128)S(1)}, f32[9,64,1]{2,1,0:T(8,128)S(1)}, u32[]{:S(2)}, u32[]{:S(2)}) collective-permute-start(f32[9,64,1]{2,1,0:T(8,128)S(1)} %get-tuple-element.33), channel_id=1, source_target_pairs={{0,1},{1,2},{2,3},{3,4},{4,5},{5,6},{6,7},{7,0},{8,9},{9,10},{10,1... | collective-permute-start | bytes 6920 | tf_op jit(solution)/shard_map/ppermute | solution.py:245
  61.9 16.0 %collective-permute-start.5 = (f32[9,64,1]{2,1,0:T(8,128)S(1)}, f32[9,64,1]{2,1,0:T(8,128)S(1)}, u32[]{:S(2)}, u32[]{:S(2)}) collective-permute-start(f32[9,64,1]{2,1,0:T(8,128)S(1)} %get-tuple-element.32), channel_id=1, source_target_pairs={{1,0},{2,1},{3,2},{4,3},{5,4},{6,5},{7,6},{0,7},{9,8},{10,9},{11,1... | collective-permute-start | bytes 6920 | tf_op jit(solution)/shard_map/ppermute | solution.py:248
  75.2 2.6 %copy-start.2 = (f32[9,64,1]{2,1,0:T(8,128)}, f32[9,64,1]{2,1,0:T(8,128)S(1)}, u32[]{:S(2)}) copy-start(f32[9,64,1]{2,1,0:T(8,128)S(1)} %collective-permute-done.4.left_ref) | copy-start | bytes 6916
  77.8 0.7 copy-start.3
  83.6 3.4 %collective-permute-start.6 = (f32[64,512]{1,0:T(8,128)}, f32[64,512]{1,0:T(8,128)S(1)}, u32[]{:S(2)}, u32[]{:S(2)}) collective-permute-start(f32[64,512]{1,0:T(8,128)} %get-tuple-element.29), channel_id=1, source_target_pairs={{8,0},{16,8},{24,16},{9,1},{17,9},{25,17},{10,2},{18,10},{26,18},{... | collective-permute-start | bytes 393224 | tf_op jit(solution)/shard_map/ppermute | solution.py:257
where the time goes:
time: 134 us; the launch traced here: 133 us
  blocking collectives  55.7 us (42%)
  Pallas kernels  35.7 us (27%)
  starting transfers between devices  15.9 us (12%)
  waiting for transfers between devices  15 us (11%)
  local copies, waits for them, and re-layouts  6.74 us (5%)
  other arithmetic  3.52 us (3%)
    all_gather x1, blocking collectives, local(): totals = jnp.sum(lax.all_gather(squares[:, :, 0], 'lon', axis=0), axis=0)  30.7 us
    all_gather x2, blocking collectives, local(): sides = lax.all_gather(side, 'lev', axis=0, tiled=True)  16.1 us
    pallas_call x1, Pallas kernels, local(): call(factor_kernel, [((inner, inner), bf16), ((inner, inner), bf16), ((2,...  10.3 us
    pallas_call x2, Pallas kernels, local(): call(forcing_kernel, [((inner, columns), f32), ((size, columns), f32), ((...  10.1 us
    all_gather x1, blocking collectives, local(): gathered = lax.all_gather(sent, 'lev', axis=0)  8.88 us
    pallas_call x1, Pallas kernels, local(): call(interface_kernel, [((levels * size, count * size), bf16)] * 2, [SMEM...  8.86 us
    ppermute x2, waiting for transfers between devices, local(): lax.ppermute(current[:, :, columns - 1:], 'lon', [(i, (i + 1) % around) f...  8.67 us
    ppermute x2, starting transfers between devices, local(): lax.ppermute(current[:, :, :1], 'lon', [((i + 1) % around, i) for i in ra...  7.81 us
  transfers between devices with their start and end apart: 7, of which 4 were waited for; matrix products, arithmetic and copies ran while one was open for 2% of the time, Pallas kernels for 14%

commit v1 on v0

--- a/solution.py
+++ b/solution.py
@@ -7,7 +7,6 @@
 from jax.experimental.pallas import tpu as pltpu
 from jax.sharding import PartitionSpec as P
 
-ITERS = 2
 HIGHEST = lax.Precision.HIGHEST
 SMEM = pl.BlockSpec(memory_space=pltpu.SMEM)
 VMEM = pl.BlockSpec(memory_space=pltpu.VMEM)
@@ -124,19 +123,20 @@
     return mul(a_high, b_high) + (mul(a_low, b_high) + mul(a_high, b_low))
 
 
-def factor_kernel(links_ref, loss_ref, high_ref, low_ref, ends_ref, send_ref):
+def factor_kernel(links_ref, top_ref, loss_ref, high_ref, low_ref, ends_ref, send_ref):
     levels, size = loss_ref.shape[0], loss_ref.shape[1]
     inner = levels - 1
     on_diag = eye_of(size)
+    top_link, inner_link = top_ref[0:1, 0:1], links_ref[inner - 1]
 
     def diag_of(k):
-        return loss_ref[k] + jnp.where(on_diag, 1.0 + links_ref[k] + links_ref[k + 1], 0.0)
+        above = top_link if k == 0 else links_ref[k - 1]
+        return loss_ref[k] + jnp.where(on_diag, 1.0 + above + links_ref[k], 0.0)
 
     def low(k, x, transposed=False, right=False):
-        return links_ref[k] * x
+        return links_ref[k - 1] * x
 
     panels = dense_inverse([diag_of(k) for k in range(inner)], low)
-    top_link, inner_link = links_ref[0], links_ref[inner]
     for k, panel in enumerate(panels):
         high, rest = split(panel)
         high_ref[:, k * size : (k + 1) * size] = high
@@ -172,48 +172,250 @@
     high_ref[length:], low_ref[length:] = split(own.T)
 
 
-def forcing_kernel(
-    links_ref, mix_ref, cur_ref, left_ref, right_ref, prev_ref, pair_ref, high_ref, low_ref,
-    part_ref, side_ref, top_ref, force_ref,
-):
+def send(src, dst, sems, slot, device):
+    return pltpu.make_async_remote_copy(
+        src_ref=src,
+        dst_ref=dst,
+        send_sem=sems.at[0, slot],
+        recv_sem=sems.at[1, slot],
+        device_id=device,
+        device_id_type=pl.DeviceIdType.MESH,
+    )
+
+
+def greet(lev_all, lon_all):
+    barrier = pltpu.get_barrier_semaphore()
+    partners = []
+    for axis, everyone in (("lev", lev_all), ("lon", lon_all)):
+        count, me = lax.axis_size(axis), lax.axis_index(axis)
+        if everyone is None:
+            continue
+        steps = range(1, count) if everyone else sorted({1, count - 1})
+        partners += [{axis: lax.rem(me + d, count)} for d in steps if d % count]
+    for device in partners:
+        pl.semaphore_signal(
+            barrier, inc=1, device_id=device, device_id_type=pl.DeviceIdType.MESH
+        )
+    pl.semaphore_wait(barrier, len(partners))
+
+
+def pack_edges(cur_ref, edges_ref):
+    levels, size, columns = cur_ref.shape
+    lane = lax.broadcasted_iota(jnp.int32, (size, 128), 1)
+    last = jnp.zeros((size, 128), jnp.float32)
+    first = last
+    for k in range(levels):
+        tail = pltpu.roll(cur_ref[k, :, columns - 128 :], k + 1, 1)
+        head = cur_ref[k, :, :128]
+        head = pltpu.roll(head, k, 1) if k else head
+        last = jnp.where(lane == k, tail, last)
+        first = jnp.where(lane == k, head, first)
+    edges_ref[0] = last
+    edges_ref[1] = first
+
+
+def halo_copies(edges_ref, halo_ref, sems):
+    around, me = lax.axis_size("lon"), lax.axis_index("lon")
+    return [
+        send(edges_ref.at[0], halo_ref.at[0], sems, 0, {"lon": lax.rem(me + 1, around)}),
+        send(edges_ref.at[1], halo_ref.at[1], sems, 1, {"lon": lax.rem(me + around - 1, around)}),
+    ]
+
+
+def local_forcing(mix_ref, cur_ref, prev_ref, pair_ref, force_ref):
     levels, size, columns = cur_ref.shape
     lane = lax.broadcasted_iota(jnp.int32, (size, columns), 1)
     for k in range(levels):
         c = cur_ref[k]
-        back = jnp.where(lane == 0, left_ref[k], pltpu.roll(c, 1, 1))
-        ahead = jnp.where(lane == columns - 1, right_ref[k], pltpu.roll(c, columns - 1, 1))
+        back = jnp.where(lane == 0, 0.0, pltpu.roll(c, 1, 1))
+        ahead = jnp.where(lane == columns - 1, 0.0, pltpu.roll(c, columns - 1, 1))
         p_high, p_low = split(pair_ref[k])
         chem = dot3(p_high, p_low, c * c)
         force_ref[k * size : (k + 1) * size] = (
             prev_ref[k] - chem + mix_ref[k] * (back + ahead - 2.0 * c)
         )
-    inner = (levels - 1) * size
-    part = dot3(high_ref[...], low_ref[...], force_ref[:inner])
-    part_ref[...] = part
-    side_ref[...] = force_ref[inner:] + links_ref[levels - 1] * part[-size:]
-    top_ref[...] = links_ref[0] * part[:size]
-
-
-def finish_kernel(part_ref, sides_ref, high_ref, low_ref, out_ref, sum_ref):
+
+
+def add_halo(mix_ref, halo_ref, force_ref):
+    levels = mix_ref.shape[0]
+    size, columns = halo_ref.shape[1], force_ref.shape[1]
+    lane = lax.broadcasted_iota(jnp.int32, (size, 128), 1)
+    before, after = halo_ref[0], halo_ref[1]
+    for k in range(levels):
+        rows = slice(k * size, (k + 1) * size)
+        at_head = pltpu.roll(before, 128 - k, 1) if k else before
+        at_tail = pltpu.roll(after, 127 - k, 1)
+        force_ref[rows, :128] += jnp.where(lane == 0, mix_ref[k] * at_head, 0.0)
+        force_ref[rows, columns - 128 :] += jnp.where(lane == 127, mix_ref[k] * at_tail, 0.0)
+
+
+def couple(
+    links_ref, top_link, g_high, g_low, force_ref, part_ref, f_high, f_low, top_out, top_in, sides_ref,
+    sems,
+):
+    count, me = lax.axis_size("lev"), lax.axis_index("lev")
+    inner, size = part_ref.shape[0], top_out.shape[0]
+    f_high[...], f_low[...] = split(force_ref[:inner])
+    mul = functools.partial(jnp.dot, preferred_element_type=jnp.float32)
+
+    def rows_of(start, stop):
+        a, b = g_high[start:stop], g_low[start:stop]
+        part = mul(a, f_high[...]) + (mul(b, f_high[...]) + mul(a, f_low[...]))
+        part_ref[start:stop] = part
+        return part
+
+    top_out[...] = top_link * rows_of(0, size)
+    sides_ref[me] = force_ref[inner:] + links_ref[inner // size - 1] * rows_of(inner - size, inner)
+    up = send(top_out, top_in, sems, 0, {"lev": lax.rem(me + count - 1, count)})
+    half = size * ((inner // size) // 2)
+
+    @pl.when(me > 0)
+    def _():
+        up.start()
+
+    rows_of(size, half)
+
+    @pl.when(me < count - 1)
+    def _():
+        up.wait_recv()
+        sides_ref[me] += top_in[...]
+
+    copies = [
+        send(sides_ref.at[me], sides_ref.at[me], sems, d, {"lev": lax.rem(me + d, count)})
+        for d in range(1, count)
+    ]
+    for copy in copies:
+        copy.start()
+    rows_of(half, inner - size)
+
+    @pl.when(me > 0)
+    def _():
+        up.wait_send()
+
+    return copies
+
+
+def finish(part_ref, sides_ref, high_ref, low_ref, out_ref):
     levels, size, columns = out_ref.shape
-    inner = (levels - 1) * size
-    x = dot3(high_ref[...], low_ref[...], sides_ref[...])
+    count = sides_ref.shape[0]
+    b_high, b_low = split(sides_ref[...].reshape(count * size, columns))
+    mul = functools.partial(jnp.dot, preferred_element_type=jnp.float32)
     for k in range(levels):
-        row = x[k * size : (k + 1) * size]
-        if k < levels - 1:
-            row = row + part_ref[k * size : (k + 1) * size]
-        out_ref[k] = row
-        sum_ref[k] = jnp.sum(row * row, axis=1, keepdims=True)
-
-
-def call(kernel, outs, places, scratch=()):
+        rows = slice(k * size, (k + 1) * size)
+        a, b = high_ref[rows], low_ref[rows]
+        row = mul(a, b_high) + (mul(b, b_high) + mul(a, b_low))
+        out_ref[k] = row + part_ref[rows] if k < levels - 1 else row
+
+
+def open_kernel(
+    links_ref, mix_ref, prev_ref, pair_ref, force_ref, top_ref, edges, halo, link_out, sems
+):
+    levels = prev_ref.shape[0]
+    count, me = lax.axis_size("lev"), lax.axis_index("lev")
+    pack_edges(prev_ref, edges)
+    link_out[...] = jnp.full(link_out.shape, links_ref[levels - 1], jnp.float32)
+    greet(False, False)
+    copies = halo_copies(edges, halo, sems)
+    down = send(link_out, top_ref, sems, 2, {"lev": lax.rem(me + 1, count)})
+    for copy in copies:
+        copy.start()
+
+    @pl.when(me < count - 1)
+    def _():
+        down.start()
+
+    @pl.when(me == 0)
+    def _():
+        top_ref[...] = jnp.zeros(top_ref.shape, jnp.float32)
+
+    local_forcing(mix_ref, prev_ref, prev_ref, pair_ref, force_ref)
+    for copy in copies:
+        copy.wait()
+    add_halo(mix_ref, halo, force_ref)
+
+    @pl.when(me < count - 1)
+    def _():
+        down.wait_send()
+
+    @pl.when(me > 0)
+    def _():
+        down.wait_recv()
+
+
+def gather_kernel(
+    links_ref, top_ref, sent_ref, force_ref, g_high, g_low, all_ref, part_ref, sides_ref,
+    f_high, f_low, top_out, top_in, sems, block_sems,
+):
+    count, me = lax.axis_size("lev"), lax.axis_index("lev")
+    greet(True, None)
+    copies = [
+        send(sent_ref, all_ref.at[me], block_sems, d, {"lev": lax.rem(me + d, count)})
+        for d in range(1, count)
+    ]
+    for copy in copies:
+        copy.start()
+    all_ref[me] = sent_ref[...]
+    copies += couple(
+        links_ref, top_ref[0:1, 0:1], g_high, g_low, force_ref, part_ref, f_high, f_low,
+        top_out, top_in, sides_ref, sems,
+    )
+    for copy in copies:
+        copy.wait()
+
+
+def newton_kernel(
+    links_ref, mix_ref, top_ref, part_in, sides_in, h_high, h_low, g_high, g_low, prev_ref, pair_ref,
+    out_ref, var_ref, cur_ref, edges, halo, force_ref, part_ref, sides_ref, f_high, f_low,
+    top_out, top_in, sums_ref, halo_sems, sems, sum_sems,
+):
+    levels, size, columns = prev_ref.shape
+    around, place = lax.axis_size("lon"), lax.axis_index("lon")
+    greet(True, True)
+    finish(part_in, sides_in, h_high, h_low, cur_ref)
+    pack_edges(cur_ref, edges)
+    copies = halo_copies(edges, halo, halo_sems)
+    for copy in copies:
+        copy.start()
+    local_forcing(mix_ref, cur_ref, prev_ref, pair_ref, force_ref)
+    for copy in copies:
+        copy.wait()
+    add_halo(mix_ref, halo, force_ref)
+    copies = couple(
+        links_ref, top_ref[0:1, 0:1], g_high, g_low, force_ref, part_ref, f_high, f_low,
+        top_out, top_in, sides_ref, sems,
+    )
+    for copy in copies:
+        copy.wait()
+    finish(part_ref, sides_ref, h_high, h_low, out_ref)
+    lane = lax.broadcasted_iota(jnp.int32, (size, 128), 1)
+    total = jnp.zeros((size, 128), jnp.float32)
+    for k in range(levels):
+        row = out_ref[k]
+        total = jnp.where(lane == k, jnp.sum(row * row, axis=1, keepdims=True), total)
+    sums_ref[0] = total
+    copies = [
+        send(sums_ref.at[0], sums_ref.at[d], sum_sems, d, {"lon": lax.rem(place + d, around)})
+        for d in range(1, around)
+    ]
+    for copy in copies:
+        copy.start()
+    for copy in copies:
+        copy.wait()
+    total = sums_ref[place]
+    for j in range(1, around):
+        total = total + sums_ref[lax.rem(place - j + around, around)]
+    var_ref[...] = (total / (columns * around)).T[:levels]
+
+
+def call(kernel, outs, places, scratch=(), group=None):
+    extra = {} if group is None else {"collective_id": group, "has_side_effects": True}
     return pl.pallas_call(
         kernel,
         out_shape=[jax.ShapeDtypeStruct(shape, dtype) for shape, dtype in outs],
         in_specs=places,
         out_specs=[VMEM] * len(outs),
         scratch_shapes=list(scratch),
-        compiler_params=pltpu.CompilerParams(vmem_limit_bytes=60 * 2**20),
+        compiler_params=pltpu.CompilerParams(vmem_limit_bytes=60 * 2**20, **extra),
     )
 
 
@@ -223,46 +425,53 @@
     around = lax.axis_size("lon")
     inner = (levels - 1) * size
     f32, bf16 = jnp.float32, jnp.bfloat16
-    top_link = lax.ppermute(
-        diffusivity[levels - 1 :], "lev", [(i, i + 1) for i in range(count - 1)]
-    )
-    links = jnp.concatenate([top_link, diffusivity])
     place = lax.axis_index("lev").astype(jnp.int32).reshape(1)
+    buf, sem = pltpu.VMEM, lambda n: pltpu.SemaphoreType.DMA((2, n))
+    force, top = call(
+        open_kernel,
+        [((levels * size, columns), f32), ((8, 128), f32)],
+        [SMEM, SMEM, VMEM, VMEM],
+        [buf((2, size, 128), f32), buf((2, size, 128), f32), buf((8, 128), f32), sem(3)],
+        0,
+    )(diffusivity, mixing, previous, pair_matrix)
     g_high, g_low, ends, sent = call(
         factor_kernel,
         [((inner, inner), bf16), ((inner, inner), bf16), ((2, inner, size), f32), ((3, size, size), f32)],
-        [SMEM, VMEM],
-    )(links, loss_matrix)
-    gathered = lax.all_gather(sent, "lev", axis=0)
+        [SMEM, VMEM, VMEM],
+    )(diffusivity, top, loss_matrix)
+    workspace = [buf((inner, columns), bf16)] * 2 + [buf((size, columns), f32)] * 2
+    gathered, part, sides = call(
+        gather_kernel,
+        [((count, 3, size, size), f32), ((inner, columns), f32), ((count, size, columns), f32)],
+        [SMEM] + [VMEM] * 5,
+        workspace + [sem(count), sem(count)],
+        1,
+    )(diffusivity, top, sent, force, g_high, g_low)
     h_high, h_low = call(
         interface_kernel,
         [((levels * size, count * size), bf16)] * 2,
         [SMEM, VMEM, VMEM],
-        [pltpu.VMEM((count, count * size, size), f32)],
+        [buf((count, count * size, size), f32)],
     )(place, gathered, ends)
-    current = previous
-    for _ in range(ITERS):
-        left = lax.ppermute(
-            current[:, :, columns - 1 :], "lon", [(i, (i + 1) % around) for i in range(around)]
-        )
-        right = lax.ppermute(
-            current[:, :, :1], "lon", [((i + 1) % around, i) for i in range(around)]
-        )
-        part, side, top = call(
-            forcing_kernel,
-            [((inner, columns), f32), ((size, columns), f32), ((size, columns), f32)],
-            [SMEM, SMEM] + [VMEM] * 7,
-            [pltpu.VMEM((levels * size, columns), f32)],
-        )(links, mixing, current, left, right, previous, pair_matrix, g_high, g_low)
-        side = side + lax.ppermute(top, "lev", [(i + 1, i) for i in range(count - 1)])
-        sides = lax.all_gather(side, "lev", axis=0, tiled=True)
-        current, squares = call(
-            finish_kernel,
-            [((levels, size, columns), f32), ((levels, size, 1), f32)],
-            [VMEM] * 4,
-        )(part, sides, h_high, h_low)
-    totals = jnp.sum(lax.all_gather(squares[:, :, 0], "lon", axis=0), axis=0)
-    return (current, totals / (columns * around))
+    return call(
+        newton_kernel,
+        [((levels, size, columns), f32), ((levels, size), f32)],
+        [SMEM, SMEM] + [VMEM] * 9,
+        [
+            buf((levels, size, columns), f32),
+            buf((2, size, 128), f32),
+            buf((2, size, 128), f32),
+            buf((levels * size, columns), f32),
+            buf((inner, columns), f32),
+            buf((count, size, columns), f32),
+            *workspace,
+            buf((around, size, 128), f32),
+            sem(2),
+            sem(count),
+            sem(around),
+        ],
+        2,
+    )(diffusivity, mixing, top, part, sides, h_high, h_low, g_high, g_low, previous, pair_matrix)
 
 
 def solution(mesh):

time: 134 us -> 79.8 us (0.60)
  blocking collectives: 55.7 us -> 0 us
  Pallas kernels: 35.7 us -> 75.8 us
  starting transfers between devices: 15.9 us -> 0 us
  waiting for transfers between devices: 15 us -> 0 us
  local copies, waits for them, and re-layouts: 6.74 us -> 2.97 us
  other arithmetic: 3.52 us -> 0 us
    all_gather x4 -> x0, blocking collectives: 55.7 us -> none  [the longest x1 30.7 us: local(): totals = jnp.sum(lax.all_gather(squares[:, :, 0], 'lon', axis=0), axis=0)]
    pallas_call x4 -> x3, Pallas kernels: 16.6 us -> 57 us  [the longest x1 29.1 us: local(): call(newton_kernel, [((levels, size, columns), f32), ((levels, size), f32...]
    ppermute x7 -> x0, starting transfers between devices: 15.9 us -> none  [the longest x2 7.81 us: local(): lax.ppermute(current[:, :, :1], 'lon', [((i + 1) % around, i) for i in ra...]
    ppermute x7 -> x0, waiting for transfers between devices: 15 us -> none  [the longest x2 8.67 us: local(): lax.ppermute(current[:, :, columns - 1:], 'lon', [(i, (i + 1) % around) f...]
    slice x3 -> x0, local copies, waits for them, and re-layouts: 3.69 us -> none  [the longest x2 2.39 us: local(): current[:, :, :1]]
    unnamed x14 -> x4, local copies, waits for them, and re-layouts: 1.44 us -> 2.97 us
  transfers between devices with their start and end apart: 7 -> 0, of which waited for: 4 -> 0; matrix products, arithmetic and copies ran while one was open for 2% -> 0% of each run, Pallas kernels for 14% -> 0%
where the time goes in v1:
time: 79.8 us; the launch traced here: 79.4 us
  Pallas kernels  75.8 us (95%)
  local copies, waits for them, and re-layouts  2.97 us (4%)
    pallas_call x1, Pallas kernels, local(): call(newton_kernel, [((levels, size, columns), f32), ((levels, size), f32...  29.1 us
    pallas_call x1, Pallas kernels, local(): call(gather_kernel, [((count, 3, size, size), f32), ((inner, columns), f3...  15.9 us
    pallas_call x1, Pallas kernels, local(): call(open_kernel, [((levels * size, columns), f32), ((8, 128), f32)], [SM...  12 us
    pallas_call x1, Pallas kernels, local(): call(factor_kernel, [((inner, inner), bf16), ((inner, inner), bf16), ((2,...  9.91 us
    pallas_call x1, Pallas kernels, local(): call(interface_kernel, [((levels * size, count * size), bf16)] * 2, [SMEM...  8.85 us
    unnamed x4, local copies, waits for them, and re-layouts  2.97 us

profile of v1, /device:TPU:0, one launch (start us, length us, event | category | flops | bytes accessed | tf_op | source)
XLA Modules:
  0.0 79.4 jit_solution(5790475279700176133)
XLA Ops:
  0.6 12.0 %shard_map.68 = (f32[576,512]{1,0:T(8,128)}, f32[8,128]{1,0:T(8,128)}) custom-call(f32[9]{0:T(128)} %links_ref.7, f32[9]{0:T(128)} %mix_ref.3, f32[9,64,512]{2,1,0:T(8,128)} %prev_ref.3, f32[9,64,64]{2,1,0:T(8,128)} %pair_ref.3), custom_call_target="tpu_custom_call" | custom-call | tf_op jit(solution)/shard_map/pallas_call | solution.py:430
  12.7 9.9 %shard_map.69 = (bf16[512,512]{1,0:T(8,128)(2,1)}, bf16[512,512]{1,0:T(8,128)(2,1)}, f32[2,512,64]{2,1,0:T(8,128)}, f32[3,64,64]{2,1,0:T(8,128)}) custom-call(f32[9]{0:T(128)} %links_ref.7, f32[8,128]{1,0:T(8,128)} %get-tuple-element.13.top_ref, f32[9,64,64]{2,1,0:T(8,128)} %loss_ref.1), custom_call_target="tpu_custom_call" | custom-call | tf_op jit(solution)/shard_map/pallas_call | solution.py:437
  22.6 15.9 %shard_map.70 = (f32[4,3,64,64]{3,2,1,0:T(8,128)}, f32[512,512]{1,0:T(8,128)}, f32[4,64,512]{2,1,0:T(8,128)}) custom-call(f32[9]{0:T(128)} %links_ref.7, f32[8,128]{1,0:T(8,128)} %get-tuple-element.13.top_ref, f32[3,64,64]{2,1,0:T(8,128)} %get-tuple-element.14.sent_ref, f32[576,512]{1,0:T(8,128)} %get-tuple-element.15.force_ref, ...), custom_call_target="tpu_custom_call" | custom-call | tf_op jit(solution)/shard_map/pallas_call | solution.py:443
  38.5 8.9 %shard_map.71 = (bf16[576,256]{1,0:T(8,128)(2,1)}, bf16[576,256]{1,0:T(8,128)(2,1)}) custom-call(s32[1]{0:T(128)} %bitcast.place_ref, f32[4,3,64,64]{3,2,1,0:T(8,128)} %get-tuple-element.20.all_ref, f32[2,512,64]{2,1,0:T(8,128)} %get-tuple-element.21.ends_ref), custom_call_target="tpu_custom_call" | custom-call | tf_op jit(solution)/shard_map/pallas_call | solution.py:450
  47.3 29.1 %shard_map.72 = (f32[9,64,512]{2,1,0:T(8,128)}, f32[9,64]{1,0:T(8,128)}) custom-call(f32[9]{0:T(128)} %links_ref.7, f32[9]{0:T(128)} %mix_ref.3, f32[8,128]{1,0:T(8,128)} %get-tuple-element.13.top_ref, f32[512,512]{1,0:T(8,128)} %get-tuple-element.18.part_in, f32[4,64,512]{2,1,0:T(8,128)} %get-tuple-element.19.sides_in, ...), custom_call_target="tpu_custom_call" | custom-call | tf_op jit(solution)/shard_map/pallas_call | solution.py:456
  76.4 0.0 copy-start
  76.4 2.4 %copy.9 = f32[9,64,512]{2,1,0:T(8,128)} copy(f32[9,64,512]{2,1,0:T(8,128)} %get-tuple-element.26) | data formatting | bytes 2359296
  78.8 0.0 copy-done
  78.8 0.6 copy.10
Async XLA Ops:
  76.4 2.4 %copy-start = (f32[9,64]{1,0:T(8,128)S(1)}, f32[9,64]{1,0:T(8,128)}, u32[]{:S(2)}) copy-start(f32[9,64]{1,0:T(8,128)} %get-tuple-element.27) | copy-start | bytes 6916

commit v2 on v1

--- a/solution.py
+++ b/solution.py
@@ -7,6 +7,8 @@
 from jax.experimental.pallas import tpu as pltpu
 from jax.sharding import PartitionSpec as P
 
+LEAST = 1.05
+MOST = 10.0
 HIGHEST = lax.Precision.HIGHEST
 SMEM = pl.BlockSpec(memory_space=pltpu.SMEM)
 VMEM = pl.BlockSpec(memory_space=pltpu.VMEM)
@@ -28,30 +30,45 @@
     return rows == cols
 
 
-def invert_all(blocks):
+def invert_all(blocks, floors, steps):
     size = blocks[0].shape[0]
-    on_diag = eye_of(size)
-    unit = jnp.where(on_diag, 1.0, 0.0).astype(jnp.float32)
+    unit = jnp.where(eye_of(size), 1.0, 0.0).astype(jnp.float32)
     start, worst = [], None
-    for a in blocks:
-        total = jnp.sum(jnp.abs(a), axis=0, keepdims=True)
-        diag = jnp.sum(jnp.where(on_diag, a, 0.0), axis=0, keepdims=True)
-        hi = jnp.max(total)
-        lo = jnp.maximum(jnp.min(2.0 * diag - total), 1.0)
+    for a, lo in zip(blocks, floors):
+        hi = jnp.max(jnp.sum(jnp.abs(a), axis=0, keepdims=True), axis=1, keepdims=True)
+        hi = jnp.clip(hi, lo, lo * spread(size))
         scale = 2.0 / (hi + lo)
         rho = (hi - lo) / (hi + lo)
-        start.append(scale * (2.0 * unit - scale * a))
+        start.append((scale, a))
         worst = rho if worst is None else jnp.maximum(worst, rho)
 
-    def go_on(carry):
-        return carry[0] > 3e-8
+    def grow(rho):
+        square = rho * rho
+        return square / (2.0 - square), 2.0 / (2.0 - square)
+
+    rho, gain = grow(worst)
+    start = [(gain * scale) * (2.0 * unit - scale * a) for scale, a in start]
 
     def step(carry):
-        bound, *xs = carry
+        rho, *xs = carry
         rest = [unit - dot(a, x) for a, x in zip(blocks, xs)]
-        return (bound * bound, *[x + dot(x, r) for x, r in zip(xs, rest)])
-
-    return lax.while_loop(go_on, step, (worst * worst, *start))[1:]
+        rho, gain = grow(rho)
+        return (rho, *[gain * (x + dot(x, r)) for x, r in zip(xs, rest)])
+
+    if steps is None:
+        return lax.while_loop(lambda carry: jnp.max(carry[0]) > 3e-8, step, (rho, *start))[1:]
+    return lax.fori_loop(0, steps, lambda i, carry: step(carry), (rho, *start))[1:]
+
+
+def spread(size):
+    return (1.0 + MOST * size) / (0.96 * LEAST)
+
+
+def enough_steps(condition):
+    rho, steps = (condition - 1.0) / (condition + 1.0), -1
+    while rho > 3e-8:
+        rho, steps = rho * rho / (2.0 - rho * rho), steps + 1
+    return steps
 
 
 def plan(lo, hi, out):
@@ -63,30 +80,43 @@
     return depth
 
 
-def dense_inverse(diag, low):
+def dense_inverse(diag, low, floor_diag, floor_low, steps=None):
     count, size = len(diag), diag[0].shape[0]
     unit = jnp.where(eye_of(size), 1.0, 0.0).astype(jnp.float32)
-    by_depth, done = {}, {}
+    by_depth, done, thin = {}, {}, {}
     plan(0, count, by_depth)
     for depth in sorted(by_depth):
         nodes = by_depth[depth]
-        schur, arms = [], []
+        schur, arms, floors, thin_arms = [], [], [], []
         for lo, mid, hi in nodes:
             s, parts = diag[mid], []
+            t, thin_parts = floor_diag[mid], []
             if lo < mid:
-                panel = done[lo, mid][-1]
-                arm = low_right(panel, low, mid, False)
+                arm = low_right(done[lo, mid][-1], low, mid, False)
                 s = s - low(mid, arm[-size:])
                 parts.append(arm)
+                thin_parts += [floor_low[mid] * x for x in thin[lo, mid][-1]]
+                t = t - floor_low[mid] * thin_parts[-1]
             parts.append(unit)
+            thin_parts.append(1.0)
             if mid + 1 < hi:
-                panel = done[mid + 1, hi][0]
-                arm = low_right(panel, low, mid + 1, True)
+                arm = low_right(done[mid + 1, hi][0], low, mid + 1, True)
                 s = s - low(mid + 1, arm[:size], True)
                 parts.append(arm)
+                thin_arm = [floor_low[mid + 1] * x for x in thin[mid + 1, hi][0]]
+                t = t - floor_low[mid + 1] * thin_arm[0]
+                thin_parts += thin_arm
             schur.append(s)
+            floors.append(t)
             arms.append(jnp.concatenate(parts, axis=0) if len(parts) > 1 else parts[0])
-        for (lo, mid, hi), v, z in zip(nodes, arms, invert_all(schur)):
+            thin_arms.append(thin_parts)
+        inverses = invert_all(schur, [0.97 * t for t in floors], steps)
+        for (lo, mid, hi), v, z, thin_v, t in zip(nodes, arms, inverses, thin_arms, floors):
+            thin[lo, hi] = [[a * b / t for b in thin_v] for a in thin_v]
+            for a, b in ((lo, mid), (mid + 1, hi)):
+                for i in range(a, b):
+                    for j in range(a, b):
+                        thin[lo, hi][i - lo][j - lo] += thin[a, b][i - a][j - a]
             if hi - lo == 1:
                 done[lo, hi] = [z]
                 continue
@@ -105,7 +135,7 @@
                     pieces.append(piece)
                 panels.append(jnp.concatenate(pieces, axis=0) if len(pieces) > 1 else pieces[0])
             done[lo, hi] = panels
-    return done[0, count]
+    return done[0, count], thin[0, count]
 
 
 def low_right(panel, low, k, plain):
@@ -127,43 +157,68 @@
     levels, size = loss_ref.shape[0], loss_ref.shape[1]
     inner = levels - 1
     on_diag = eye_of(size)
-    top_link, inner_link = top_ref[0:1, 0:1], links_ref[inner - 1]
+    top_link, inner_link = top_ref[0:1, 0:1], jnp.full((1, 1), links_ref[inner - 1])
+    links = [jnp.full((1, 1), links_ref[k]) for k in range(levels)]
 
     def diag_of(k):
-        above = top_link if k == 0 else links_ref[k - 1]
-        return loss_ref[k] + jnp.where(on_diag, 1.0 + above + links_ref[k], 0.0)
+        above = top_link if k == 0 else links[k - 1]
+        return loss_ref[k] + jnp.where(on_diag, 1.0 + above + links[k], 0.0)
 
     def low(k, x, transposed=False, right=False):
         return links_ref[k - 1] * x
 
-    panels = dense_inverse([diag_of(k) for k in range(inner)], low)
+    floor_diag = [
+        LEAST + links[k] + (top_link if k == 0 else links[k - 1]) for k in range(levels)
+    ]
+    panels, thin = dense_inverse(
+        [diag_of(k) for k in range(inner)], low, floor_diag[:inner], [top_link] + links[: inner - 1]
+    )
     for k, panel in enumerate(panels):
         high, rest = split(panel)
         high_ref[:, k * size : (k + 1) * size] = high
         low_ref[:, k * size : (k + 1) * size] = rest
     ends_ref[0] = top_link * panels[0]
     ends_ref[1] = inner_link * panels[-1]
-    send_ref[0] = diag_of(inner) - inner_link * inner_link * panels[-1][-size:]
-    send_ref[1] = top_link * top_link * panels[0][:size]
-    send_ref[2] = inner_link * top_link * panels[0][-size:]
-
-
-def interface_kernel(place_ref, all_ref, ends_ref, high_ref, low_ref, rows_ref):
-    count, size = all_ref.shape[0], all_ref.shape[2]
-    diag = [
-        all_ref[k, 0] - all_ref[k + 1, 1] if k + 1 < count else all_ref[k, 0]
-        for k in range(count)
+    blocks = [
+        (
+            diag_of(inner) - inner_link * inner_link * panels[-1][-size:],
+            floor_diag[inner] - inner_link * inner_link * thin[-1][-1],
+        ),
+        (top_link * top_link * panels[0][:size], top_link * top_link * thin[0][0]),
+        (inner_link * top_link * panels[0][-size:], inner_link * top_link * thin[0][-1]),
     ]
+    for k, (block, floor) in enumerate(blocks):
+        send_ref[k, :size] = block
+        send_ref[k, size:] = jnp.broadcast_to(floor, (8, size))
+
+
+def interface(all_ref, ends_ref, high_ref, low_ref, rows_ref):
+    count, size = all_ref.shape[0], all_ref.shape[3]
+
+    def diag_of(rows, cols):
+        own = [all_ref[k, 0, rows, cols] for k in range(count)]
+        return [
+            own[k] - all_ref[k + 1, 1, rows, cols] if k + 1 < count else own[k]
+            for k in range(count)
+        ]
 
     def low(k, x, transposed=False, right=False):
-        block = all_ref[k, 2]
+        block = all_ref[k, 2, :size]
         if right:
             return dot_t(x, block) if transposed else dot(x, block)
         return dot(block, x, ((0,), (0,))) if transposed else dot(block, x)
 
-    for k, panel in enumerate(dense_inverse(diag, low)):
+    thin = slice(size, size + 1), slice(0, 1)
+    panels, _ = dense_inverse(
+        diag_of(slice(0, size), slice(0, size)),
+        low,
+        diag_of(*thin),
+        [all_ref[k, 2, thin[0], thin[1]] for k in range(count)],
+        enough_steps(spread(size)),
+    )
+    for k, panel in enumerate(panels):
         rows_ref[k] = panel
-    me = place_ref[0]
+    me = lax.axis_index("lev")
     own = rows_ref[me]
     above = rows_ref[jnp.maximum(me - 1, 0)]
     inner = dot_t(ends_ref[0], above) + dot_t(ends_ref[1], own)
@@ -342,36 +397,33 @@
         down.wait_recv()
 
 
-def gather_kernel(
-    links_ref, top_ref, sent_ref, force_ref, g_high, g_low, all_ref, part_ref, sides_ref,
-    f_high, f_low, top_out, top_in, sems, block_sems,
+def newton_kernel(
+    links_ref, mix_ref, top_ref, sent_ref, ends_ref, first_force, g_high, g_low, prev_ref, pair_ref,
+    out_ref, var_ref, all_ref, rows_ref, h_high, h_low, cur_ref, edges, halo, force_ref, part_ref,
+    first_sides, sides_ref, f_high, f_low, first_out, first_in, top_out, top_in, sums_ref,
+    block_sems, first_sems, halo_sems, sems, sum_sems,
 ):
+    levels, size, columns = prev_ref.shape
     count, me = lax.axis_size("lev"), lax.axis_index("lev")
-    greet(True, None)
-    copies = [
+    around, place = lax.axis_size("lon"), lax.axis_index("lon")
+    greet(True, True)
+    blocks = [
         send(sent_ref, all_ref.at[me], block_sems, d, {"lev": lax.rem(me + d, count)})
         for d in range(1, count)
     ]
-    for copy in copies:
+    for copy in blocks:
         copy.start()
     all_ref[me] = sent_ref[...]
-    copies += couple(
-        links_ref, top_ref[0:1, 0:1], g_high, g_low, force_ref, part_ref, f_high, f_low,
-        top_out, top_in, sides_ref, sems,
-    )
-    for copy in copies:
+    copies = couple(
+        links_ref, top_ref[0:1, 0:1], g_high, g_low, first_force, part_ref, f_high, f_low,
+        first_out, first_in, first_sides, first_sems,
+    )
+    for copy in blocks:
         copy.wait()
-
-
-def newton_kernel(
-    links_ref, mix_ref, top_ref, part_in, sides_in, h_high, h_low, g_high, g_low, prev_ref, pair_ref,
-    out_ref, var_ref, cur_ref, edges, halo, force_ref, part_ref, sides_ref, f_high, f_low,
-    top_out, top_in, sums_ref, halo_sems, sems, sum_sems,
-):
-    levels, size, columns = prev_ref.shape
-    around, place = lax.axis_size("lon"), lax.axis_index("lon")
-    greet(True, True)
-    finish(part_in, sides_in, h_high, h_low, cur_ref)
+    interface(all_ref, ends_ref, h_high, h_low, rows_ref)
+    for copy in copies:
+        copy.wait()
+    finish(part_ref, first_sides, h_high, h_low, cur_ref)
     pack_edges(cur_ref, edges)
     copies = halo_copies(edges, halo, halo_sems)
     for copy in copies:
@@ -425,7 +477,6 @@
     around = lax.axis_size("lon")
     inner = (levels - 1) * size
     f32, bf16 = jnp.float32, jnp.bfloat16
-    place = lax.axis_index("lev").astype(jnp.int32).reshape(1)
     buf, sem = pltpu.VMEM, lambda n: pltpu.SemaphoreType.DMA((2, n))
     force, top = call(
         open_kernel,
@@ -436,42 +487,40 @@
     )(diffusivity, mixing, previous, pair_matrix)
     g_high, g_low, ends, sent = call(
         factor_kernel,
-        [((inner, inner), bf16), ((inner, inner), bf16), ((2, inner, size), f32), ((3, size, size), f32)],
+        [((inner, inner), bf16), ((inner, inner), bf16), ((2, inner, size), f32), ((3, size + 8, size), f32)],
         [SMEM, VMEM, VMEM],
     )(diffusivity, top, loss_matrix)
-    workspace = [buf((inner, columns), bf16)] * 2 + [buf((size, columns), f32)] * 2
-    gathered, part, sides = call(
-        gather_kernel,
-        [((count, 3, size, size), f32), ((inner, columns), f32), ((count, size, columns), f32)],
-        [SMEM] + [VMEM] * 5,
-        workspace + [sem(count), sem(count)],
-        1,
-    )(diffusivity, top, sent, force, g_high, g_low)
-    h_high, h_low = call(
-        interface_kernel,
-        [((levels * size, count * size), bf16)] * 2,
-        [SMEM, VMEM, VMEM],
-        [buf((count, count * size, size), f32)],
-    )(place, gathered, ends)
     return call(
         newton_kernel,
         [((levels, size, columns), f32), ((levels, size), f32)],
-        [SMEM, SMEM] + [VMEM] * 9,
+        [SMEM, SMEM] + [VMEM] * 8,
         [
+            buf((count, 3, size + 8, size), f32),
+            buf((count, count * size, size), f32),
+            buf((levels * size, count * size), bf16),
+            buf((levels * size, count * size), bf16),
             buf((levels, size, columns), f32),
             buf((2, size, 128), f32),
             buf((2, size, 128), f32),
             buf((levels * size, columns), f32),
             buf((inner, columns), f32),
             buf((count, size, columns), f32),
-            *workspace,
+            buf((count, size, columns), f32),
+            buf((inner, columns), bf16),
+            buf((inner, columns), bf16),
+            buf((size, columns), f32),
+            buf((size, columns), f32),
+            buf((size, columns), f32),
+            buf((size, columns), f32),
             buf((around, size, 128), f32),
+            sem(count),
+            sem(count),
             sem(2),
             sem(count),
             sem(around),
         ],
-        2,
-    )(diffusivity, mixing, top, part, sides, h_high, h_low, g_high, g_low, previous, pair_matrix)
+        1,
+    )(diffusivity, mixing, top, sent, ends, force, g_high, g_low, previous, pair_matrix)
 
 
 def solution(mesh):

time: 79.8 us -> 73.5 us (0.921)
  Pallas kernels: 75.8 us -> 68.9 us
    pallas_call x2 -> x0, Pallas kernels: 24.7 us -> none  [the longest x1 15.9 us: local(): call(gather_kernel, [((count, 3, size, size), f32), ((inner, columns), f3...]
    pallas_call x1, Pallas kernels: 29.1 us -> 47.5 us  [local(): call(newton_kernel, [((levels, size, columns), f32), ((levels, size), f32...]
where the time goes in v2:
time: 73.5 us; the launch traced here: 72.6 us
  Pallas kernels  68.9 us (94%)
  local copies, waits for them, and re-layouts  2.97 us (4%)
    pallas_call x1, Pallas kernels, local(): call(newton_kernel, [((levels, size, columns), f32), ((levels, size), f32...  47.5 us
    pallas_call x1, Pallas kernels, local(): call(open_kernel, [((levels * size, columns), f32), ((8, 128), f32)], [SM...  12 us
    pallas_call x1, Pallas kernels, local(): call(factor_kernel, [((inner, inner), bf16), ((inner, inner), bf16), ((2,...  9.36 us
    unnamed x4, local copies, waits for them, and re-layouts  2.97 us

profile of v2, /device:TPU:0, one launch (start us, length us, event | category | flops | bytes accessed | tf_op | source)
XLA Modules:
  0.0 72.6 jit_solution(13592020134215077639)
XLA Ops:
  0.6 12.0 %shard_map.68 = (f32[576,512]{1,0:T(8,128)}, f32[8,128]{1,0:T(8,128)}) custom-call(f32[9]{0:T(128)} %links_ref.5, f32[9]{0:T(128)} %mix_ref.3, f32[9,64,512]{2,1,0:T(8,128)} %prev_ref.3, f32[9,64,64]{2,1,0:T(8,128)} %pair_ref.3), custom_call_target="tpu_custom_call" | custom-call | tf_op jit(solution)/shard_map/pallas_call | solution.py:481
  12.7 9.4 %shard_map.69 = (bf16[512,512]{1,0:T(8,128)(2,1)}, bf16[512,512]{1,0:T(8,128)(2,1)}, f32[2,512,64]{2,1,0:T(8,128)}, f32[3,72,64]{2,1,0:T(8,128)}) custom-call(f32[9]{0:T(128)} %links_ref.5, f32[8,128]{1,0:T(8,128)} %get-tuple-element.8.top_ref, f32[9,64,64]{2,1,0:T(8,128)} %loss_ref.1), custom_call_target="tpu_custom_call" | custom-call | tf_op jit(solution)/shard_map/pallas_call | solution.py:488
  22.0 47.5 %shard_map.70 = (f32[9,64,512]{2,1,0:T(8,128)}, f32[9,64]{1,0:T(8,128)}) custom-call(f32[9]{0:T(128)} %links_ref.5, f32[9]{0:T(128)} %mix_ref.3, f32[8,128]{1,0:T(8,128)} %get-tuple-element.8.top_ref, f32[3,72,64]{2,1,0:T(8,128)} %get-tuple-element.9.sent_ref, f32[2,512,64]{2,1,0:T(8,128)} %get-tuple-element.10.ends_ref, ...), custom_call_target="tpu_custom_call" | custom-call | tf_op jit(solution)/shard_map/pallas_call | solution.py:493
  69.6 0.0 copy-start
  69.6 2.4 %copy.9 = f32[9,64,512]{2,1,0:T(8,128)} copy(f32[9,64,512]{2,1,0:T(8,128)} %get-tuple-element.16) | data formatting | bytes 2359296
  71.9 0.0 copy-done
  72.0 0.6 copy.10
Async XLA Ops:
  69.6 2.4 %copy-start = (f32[9,64]{1,0:T(8,128)S(1)}, f32[9,64]{1,0:T(8,128)}, u32[]{:S(2)}) copy-start(f32[9,64]{1,0:T(8,128)} %get-tuple-element.17) | copy-start | bytes 6916

commit v3 on v2

--- a/solution.py
+++ b/solution.py
@@ -444,7 +444,7 @@
     for k in range(levels):
         row = out_ref[k]
         total = jnp.where(lane == k, jnp.sum(row * row, axis=1, keepdims=True), total)
-    sums_ref[0] = total
+    sums_ref[0] = total.T[: sums_ref.shape[1]]
     copies = [
         send(sums_ref.at[0], sums_ref.at[d], sum_sems, d, {"lon": lax.rem(place + d, around)})
         for d in range(1, around)
@@ -456,7 +456,7 @@
     total = sums_ref[place]
     for j in range(1, around):
         total = total + sums_ref[lax.rem(place - j + around, around)]
-    var_ref[...] = (total / (columns * around)).T[:levels]
+    var_ref[...] = (total / (columns * around))[:levels]
 
 
 def call(kernel, outs, places, scratch=(), group=None):
@@ -512,7 +512,7 @@
             buf((size, columns), f32),
             buf((size, columns), f32),
             buf((size, columns), f32),
-            buf((around, size, 128), f32),
+            buf((around, -(-levels // 8) * 8, size), f32),
             sem(count),
             sem(count),
             sem(2),

time: 73.5 us -> 72.9 us (level); the launches traced: 72.6 us -> 73.1 us
  no operation moved by 1% of the time
where the time goes in v3:
time: 72.9 us; the launch traced here: 73.1 us
  Pallas kernels  69.5 us (95%)
  local copies, waits for them, and re-layouts  2.97 us (4%)
    pallas_call x1, Pallas kernels, local(): call(newton_kernel, [((levels, size, columns), f32), ((levels, size), f32...  48 us
    pallas_call x1, Pallas kernels, local(): call(open_kernel, [((levels * size, columns), f32), ((8, 128), f32)], [SM...  12 us
    pallas_call x1, Pallas kernels, local(): call(factor_kernel, [((inner, inner), bf16), ((inner, inner), bf16), ((2,...  9.43 us
    unnamed x4, local copies, waits for them, and re-layouts  2.97 us

profile of v3, /device:TPU:0, one launch (start us, length us, event | category | flops | bytes accessed | tf_op | source)
XLA Modules:
  0.0 73.1 jit_solution(14393193193018531263)
XLA Ops:
  0.6 12.0 %shard_map.68 = (f32[576,512]{1,0:T(8,128)}, f32[8,128]{1,0:T(8,128)}) custom-call(f32[9]{0:T(128)} %links_ref.5, f32[9]{0:T(128)} %mix_ref.3, f32[9,64,512]{2,1,0:T(8,128)} %prev_ref.3, f32[9,64,64]{2,1,0:T(8,128)} %pair_ref.3), custom_call_target="tpu_custom_call" | custom-call | tf_op jit(solution)/shard_map/pallas_call | solution.py:481
  12.7 9.4 %shard_map.69 = (bf16[512,512]{1,0:T(8,128)(2,1)}, bf16[512,512]{1,0:T(8,128)(2,1)}, f32[2,512,64]{2,1,0:T(8,128)}, f32[3,72,64]{2,1,0:T(8,128)}) custom-call(f32[9]{0:T(128)} %links_ref.5, f32[8,128]{1,0:T(8,128)} %get-tuple-element.8.top_ref, f32[9,64,64]{2,1,0:T(8,128)} %loss_ref.1), custom_call_target="tpu_custom_call" | custom-call | tf_op jit(solution)/shard_map/pallas_call | solution.py:488
  22.1 48.0 %shard_map.70 = (f32[9,64,512]{2,1,0:T(8,128)}, f32[9,64]{1,0:T(8,128)}) custom-call(f32[9]{0:T(128)} %links_ref.5, f32[9]{0:T(128)} %mix_ref.3, f32[8,128]{1,0:T(8,128)} %get-tuple-element.8.top_ref, f32[3,72,64]{2,1,0:T(8,128)} %get-tuple-element.9.sent_ref, f32[2,512,64]{2,1,0:T(8,128)} %get-tuple-element.10.ends_ref, ...), custom_call_target="tpu_custom_call" | custom-call | tf_op jit(solution)/shard_map/pallas_call | solution.py:493
  70.1 0.0 copy-start
  70.1 2.4 %copy.9 = f32[9,64,512]{2,1,0:T(8,128)} copy(f32[9,64,512]{2,1,0:T(8,128)} %get-tuple-element.16) | data formatting | bytes 2359296
  72.5 0.0 copy-done
  72.5 0.6 copy.10
Async XLA Ops:
  70.1 2.4 %copy-start = (f32[9,64]{1,0:T(8,128)S(1)}, f32[9,64]{1,0:T(8,128)}, u32[]{:S(2)}) copy-start(f32[9,64]{1,0:T(8,128)} %get-tuple-element.17) | copy-start | bytes 6916

commit v4 on v3

--- a/solution.py
+++ b/solution.py
@@ -306,7 +306,7 @@
 
 def couple(
     links_ref, top_link, g_high, g_low, force_ref, part_ref, f_high, f_low, top_out, top_in, sides_ref,
-    sems,
+    sems, direct,
 ):
     count, me = lax.axis_size("lev"), lax.axis_index("lev")
     inner, size = part_ref.shape[0], top_out.shape[0]
@@ -335,11 +335,18 @@
         up.wait_recv()
         sides_ref[me] += top_in[...]
 
+    partner = me + 1 - 2 * lax.rem(me, 2)
     copies = [
         send(sides_ref.at[me], sides_ref.at[me], sems, d, {"lev": lax.rem(me + d, count)})
-        for d in range(1, count)
+        for d in range(1 if direct else 2, count, 1 if direct else 2)
     ]
-    for copy in copies:
+    onward = [] if direct else [send(sides_ref.at[me], sides_ref.at[me], sems, 1, {"lev": partner})]
+    for d in range(count if direct else 2, count, 2):
+        origin = lax.rem(me - d + count, count)
+        onward.append(
+            send(sides_ref.at[origin], sides_ref.at[origin], sems, d + 1, {"lev": partner})
+        )
+    for copy in copies + onward[:1]:
         copy.start()
     rows_of(half, inner - size)
 
@@ -347,7 +354,17 @@
     def _():
         up.wait_send()
 
-    return copies
+    return copies, onward
+
+
+def relay(copies, onward):
+    for copy, later in zip(copies, onward[1:]):
+        copy.wait_recv()
+        later.start()
+    for copy in copies:
+        copy.wait_send()
+    for copy in onward:
+        copy.wait()
 
 
 def finish(part_ref, sides_ref, high_ref, low_ref, out_ref):
@@ -416,12 +433,12 @@
     all_ref[me] = sent_ref[...]
     copies = couple(
         links_ref, top_ref[0:1, 0:1], g_high, g_low, first_force, part_ref, f_high, f_low,
-        first_out, first_in, first_sides, first_sems,
+        first_out, first_in, first_sides, first_sems, True,
     )
     for copy in blocks:
         copy.wait()
     interface(all_ref, ends_ref, h_high, h_low, rows_ref)
-    for copy in copies:
+    for copy in copies[0]:
         copy.wait()
     finish(part_ref, first_sides, h_high, h_low, cur_ref)
     pack_edges(cur_ref, edges)
@@ -434,10 +451,9 @@
     add_halo(mix_ref, halo, force_ref)
     copies = couple(
         links_ref, top_ref[0:1, 0:1], g_high, g_low, force_ref, part_ref, f_high, f_low,
-        top_out, top_in, sides_ref, sems,
-    )
-    for copy in copies:
-        copy.wait()
+        top_out, top_in, sides_ref, sems, False,
+    )
+    relay(*copies)
     finish(part_ref, sides_ref, h_high, h_low, out_ref)
     lane = lax.broadcasted_iota(jnp.int32, (size, 128), 1)
     total = jnp.zeros((size, 128), jnp.float32)

time: 72.9 us -> 71.8 us (0.985)
  Pallas kernels: 69.5 us -> 68 us
    pallas_call x1, Pallas kernels: 48 us -> 46.6 us  [local(): call(newton_kernel, [((levels, size, columns), f32), ((levels, size), f32...]
where the time goes in v4:
time: 71.8 us; the launch traced here: 71.6 us
  Pallas kernels  68 us (95%)
  local copies, waits for them, and re-layouts  2.97 us (4%)
    pallas_call x1, Pallas kernels, local(): call(newton_kernel, [((levels, size, columns), f32), ((levels, size), f32...  46.6 us
    pallas_call x1, Pallas kernels, local(): call(open_kernel, [((levels * size, columns), f32), ((8, 128), f32)], [SM...  12 us
    pallas_call x1, Pallas kernels, local(): call(factor_kernel, [((inner, inner), bf16), ((inner, inner), bf16), ((2,...  9.36 us
    unnamed x4, local copies, waits for them, and re-layouts  2.97 us

profile of v4, /device:TPU:0, one launch (start us, length us, event | category | flops | bytes accessed | tf_op | source)
XLA Modules:
  0.0 71.6 jit_solution(5210332782697722564)
XLA Ops:
  0.6 12.0 %shard_map.68 = (f32[576,512]{1,0:T(8,128)}, f32[8,128]{1,0:T(8,128)}) custom-call(f32[9]{0:T(128)} %links_ref.5, f32[9]{0:T(128)} %mix_ref.3, f32[9,64,512]{2,1,0:T(8,128)} %prev_ref.3, f32[9,64,64]{2,1,0:T(8,128)} %pair_ref.3), custom_call_target="tpu_custom_call" | custom-call | tf_op jit(solution)/shard_map/pallas_call | solution.py:497
  12.7 9.4 %shard_map.69 = (bf16[512,512]{1,0:T(8,128)(2,1)}, bf16[512,512]{1,0:T(8,128)(2,1)}, f32[2,512,64]{2,1,0:T(8,128)}, f32[3,72,64]{2,1,0:T(8,128)}) custom-call(f32[9]{0:T(128)} %links_ref.5, f32[8,128]{1,0:T(8,128)} %get-tuple-element.8.top_ref, f32[9,64,64]{2,1,0:T(8,128)} %loss_ref.1), custom_call_target="tpu_custom_call" | custom-call | tf_op jit(solution)/shard_map/pallas_call | solution.py:504
  22.0 46.6 %shard_map.70 = (f32[9,64,512]{2,1,0:T(8,128)}, f32[9,64]{1,0:T(8,128)}) custom-call(f32[9]{0:T(128)} %links_ref.5, f32[9]{0:T(128)} %mix_ref.3, f32[8,128]{1,0:T(8,128)} %get-tuple-element.8.top_ref, f32[3,72,64]{2,1,0:T(8,128)} %get-tuple-element.9.sent_ref, f32[2,512,64]{2,1,0:T(8,128)} %get-tuple-element.10.ends_ref, ...), custom_call_target="tpu_custom_call" | custom-call | tf_op jit(solution)/shard_map/pallas_call | solution.py:509
  68.6 0.0 copy-start
  68.6 2.4 %copy.9 = f32[9,64,512]{2,1,0:T(8,128)} copy(f32[9,64,512]{2,1,0:T(8,128)} %get-tuple-element.16) | data formatting | bytes 2359296
  71.0 0.0 copy-done
  71.0 0.6 copy.10
Async XLA Ops:
  68.6 2.4 %copy-start = (f32[9,64]{1,0:T(8,128)S(1)}, f32[9,64]{1,0:T(8,128)}, u32[]{:S(2)}) copy-start(f32[9,64]{1,0:T(8,128)} %get-tuple-element.17) | copy-start | bytes 6916
